TPU v7x, 32 devices: a whole 2x2x4 slice. The times are simulated.
32 devices in a mesh: heads: 2 (over y), ctx: 16 (over z, x, core).
Axes of the slice: x: 2, y: 2, z: 4, core: 2. Of those that a mesh axis runs over, the one named last changes fastest.
Arguments:
- queries: bfloat16 [64, 8192], P('ctx', 'heads'), may hold values from -6 to 6
- keys: bfloat16 [32768, 1024], P('ctx', 'heads'), may hold values from -18 to 18
- values: bfloat16 [32768, 1024], P('ctx', 'heads'), may hold values from -6 to 6
- cache_positions: int32 [32768], P('ctx'), may hold values from 0 to 32767, as said below
- query_positions: int32 [64], P('ctx'), may hold values from 32704 to 32767, as said below
- lengths: int32 [16], P('ctx'), may hold values from 1024 to 2048, as said below
Outputs:
- attended: bfloat16 [64, 8192], P('ctx', 'heads')
Inputs may be any that keep to these rules, and one draw needn't show every extreme that they name: `cache_positions`: the values 0 to 32767, each once; slot 0 holds position 0. `query_positions`: the last 64 positions, each once. `lengths`: some block of the cache is full.
All inputs are finite; a program needn't handle non-finite values.
Results may differ from a plain program's by a relative error of at most 0.0055.
Values may be sent and summed in bfloat16 or wider, within the bound.
A program may use at most 64 MiB of HBM per device.

v0:
```python
import math

import jax
import jax.numpy as jnp
from jax import lax
from jax.sharding import PartitionSpec as P

HD = 128
GROUP = 8


NEG_FILL = -1e30


def attend_block(block, places, keys, values, key_places, live_slots):
    tok_rows = block.shape[0]
    cache_rows = keys.shape[0]
    kv_local = places.shape[0]
    q_split = block.reshape(tok_rows, kv_local, GROUP, HD)
    k_split = keys.reshape(cache_rows, kv_local, HD)
    v_split = values.reshape(cache_rows, kv_local, HD)
    scores = jnp.einsum(
        "rhgd,chd->hgrc", q_split, k_split, preferred_element_type=jnp.float32
    ) * HD ** (-0.5)
    allowed = live_slots[None, None, :] & (key_places[None, None, :] <= places[:, :, None])
    allowed = allowed[:, None]
    scores = jnp.where(allowed, scores, NEG_FILL)
    row_max = jnp.max(scores, axis=3)
    weights = jnp.where(allowed, jnp.exp(scores - row_max[..., None]), 0.0)
    row_sum = jnp.sum(weights, axis=3)
    weighted = jnp.einsum(
        "hgrc,chd->rhgd", weights.astype(jnp.bfloat16), v_split, preferred_element_type=jnp.float32
    )
    row_max = row_max.transpose(2, 0, 1).reshape(tok_rows, kv_local * GROUP)
    row_sum = row_sum.transpose(2, 0, 1).reshape(tok_rows, kv_local * GROUP)
    return (row_max, row_sum, weighted.reshape(tok_rows, kv_local * GROUP * HD))


def finish(state):
    tok_rows = state[0].shape[0]
    stat_cols = state[0].shape[1]
    result = state[2].reshape(tok_rows, stat_cols, HD) / state[1][..., None]
    return result.reshape(tok_rows, stat_cols * HD).astype(jnp.bfloat16)


def per_device(queries, keys, values, cache_positions, query_positions, lengths):
    tok_rows = queries.shape[0]
    kv_local = keys.shape[1] // HD
    live_slots = jnp.arange(keys.shape[0], dtype=jnp.int32) < lengths[0]
    cycle_size = lax.axis_size("ctx")
    everyone_places = lax.all_gather(query_positions, "ctx", axis=0, tiled=True)

    def attend_here(block, places):
        return attend_block(block, places, keys, values, cache_positions, live_slots)

    everyone = lax.all_gather(queries, "ctx", axis=0, tiled=True)
    turns = math.gcd(cycle_size, 8)
    span = everyone.shape[0] // turns

    def one_block(member):
        block, places = member
        return attend_here(block, jnp.broadcast_to(places[None, :], (kv_local, span)))

    parts = lax.map(
        one_block,
        (everyone.reshape(turns, span, everyone.shape[1]), everyone_places.reshape(turns, span)),
    )
    parts = tuple((piece.reshape(cycle_size, tok_rows, piece.shape[-1]) for piece in parts))
    home = lax.all_to_all(parts, "ctx", split_axis=0, concat_axis=0, tiled=True)
    row_max = jnp.max(home[0], axis=0)
    factors = jnp.exp(home[0] - row_max[None])
    row_sum = jnp.sum(home[1] * factors, axis=0)
    weighted = home[2].reshape(cycle_size, tok_rows, factors.shape[2], HD) * factors[..., None]
    weighted = jnp.sum(weighted, axis=0).reshape(tok_rows, factors.shape[2] * HD)
    state = (row_max, row_sum, weighted)
    return finish(state)


def solution(mesh):
    in_specs = (
        P("ctx", "heads"),
        P("ctx", "heads"),
        P("ctx", "heads"),
        P("ctx"),
        P("ctx"),
        P("ctx"),
    )
    out_specs = P("ctx", "heads")
    return jax.shard_map(
        per_device, mesh=mesh, in_specs=in_specs, out_specs=out_specs, check_vma=False
    )
```

profile of v0, /device:TPU:0, one launch (start us, length us, event | category | flops | bytes accessed | tf_op | source)
XLA Modules:
  0.0 148.7 jit_solution(7927235756383579396)
XLA Ops:
  0.0 1.3 dynamic-slice
  2.0 0.9 dynamic-update-slice
  2.9 13.7 %all-reduce = s32[64]{0:T(128)S(1)} all-reduce(s32[64]{0:T(128)S(1)} %dynamic-update-slice), channel_id=1, replica_groups=mesh['heads'=2,'ctx'=16] {'ctx'}, use_global_device_ids=true, to_apply=%add | all-reduce | flops 64 | bytes 512
  16.7 19.6 %all-gather = bf16[16,4,4096]{2,1,0:T(4,128)(2,1)S(1)} all-gather(bf16[1,4,4096]{2,1,0:T(4,128)(2,1)} %bitcast.60), channel_id=1, replica_groups=mesh['heads'=2,'ctx'=16] {'ctx'}, dimensions={0}, use_global_device_ids=true | all-gather | bytes 557056 | tf_op jit(solution)/shard_map/all_gather | solution.py:56
  36.5 4.1 %reshape.69 = bf16[2048,4,128]{2,1,0:T(4,128)(2,1)} reshape(bf16[2048,512]{1,0:T(8,128)(2,1)} %param.9) | data formatting | bytes 4194304 | tf_op jit(solution)/shard_map/while/body/eval_jaxpr/reshape | solution.py:20
  40.6 2.0 %reshape.70 = bf16[2048,4,128]{2,1,0:T(4,128)(2,1)} reshape(bf16[2048,512]{1,0:T(8,128)(2,1)S(1)} %copy-done) | data formatting | bytes 4194304 | tf_op jit(solution)/shard_map/while/body/eval_jaxpr/reshape | solution.py:21
  42.6 58.2 %while.16 = (s32[]{:T(128)}, f32[8,8,32]{2,1,0:T(8,128)S(1)}, f32[8,8,32]{2,1,0:T(8,128)S(1)}, f32[8,8,4096]{2,1,0:T(8,128)}, s32[2048]{0:T(1024)S(1)}, /*index=...) while((s32[]{:T(128)}, f32[8,8,32]{2,1,0:T(8,128)S(1)}, ...), condition=%wide.wide.region_3.4_spmd.clone, body=%wide.wide.region_0.3_spmd.clone.sunk | while | flops 273286656 | bytes 11903225 | solution.py:64
  43.4 2.6 %fusion.36 = (f32[4,8,8]{1,2,0:T(8,128)S(1)}, f32[4,8,8,2048]{3,1,2,0:T(8,128)S(1)}) fusion(bf16[2048,4,128,1]{2,1,0,3:T(4,128)(2,1)} %bitcast.53, pred[4,8,2048]{2,1,0:T(8,128)(4,1)S(1)} %compare_and_fusion.3, bf16[1,8,32,128]{3,1,2,0:T(8,128)(2,1)S(1)} %dynamic-slice_bitcast_fusion.3), kind=kOutput, calls=%fused_computation.31.clone.clone.1 | convolution fusion | flops 135790336 | bytes 4326400 | tf_op jit(solution)/shard_map/while/body/eval_jaxpr/rhgd,chd->hgrc/dot_general | solution.py:22
  46.8 2.4 %fusion.38 = f32[8,4,8,128]{3,2,0,1:T(8,128)S(1)} fusion(bf16[2048,4,128,1]{2,1,0,3:T(4,128)(2,1)} %bitcast.58, f32[4,8,8,2048]{3,1,2,0:T(8,128)S(1)} %get-tuple-element.231, f32[4,8,8]{1,2,0:T(8,128)S(1)} %get-tuple-element.232, pred[4,8,2048]{2,1,0:T(8,128)(4,1)S(1)} %compare_and_fusion.3), kind=kOutput, calls=%fused_computation.10.clone.clone.1 | convolution fusion | flops 135790592 | bytes 4391936 | tf_op jit(solution)/shard_map/while/body/eval_jaxpr/hgrc,chd->rhgd/dot_general | solution.py:31
  50.7 2.6 %fusion.36 = (f32[4,8,8]{1,2,0:T(8,128)S(1)}, f32[4,8,8,2048]{3,1,2,0:T(8,128)S(1)}) fusion(bf16[2048,4,128,1]{2,1,0,3:T(4,128)(2,1)} %bitcast.53, pred[4,8,2048]{2,1,0:T(8,128)(4,1)S(1)} %compare_and_fusion.3, bf16[1,8,32,128]{3,1,2,0:T(8,128)(2,1)S(1)} %dynamic-slice_bitcast_fusion.3), kind=kOutput, calls=%fused_computation.31.clone.clone.1 | convolution fusion | flops 135790336 | bytes 4326400 | tf_op jit(solution)/shard_map/while/body/eval_jaxpr/rhgd,chd->hgrc/dot_general | solution.py:22
  54.1 2.4 %fusion.38 = f32[8,4,8,128]{3,2,0,1:T(8,128)S(1)} fusion(bf16[2048,4,128,1]{2,1,0,3:T(4,128)(2,1)} %bitcast.58, f32[4,8,8,2048]{3,1,2,0:T(8,128)S(1)} %get-tuple-element.231, f32[4,8,8]{1,2,0:T(8,128)S(1)} %get-tuple-element.232, pred[4,8,2048]{2,1,0:T(8,128)(4,1)S(1)} %compare_and_fusion.3), kind=kOutput, calls=%fused_computation.10.clone.clone.1 | convolution fusion | flops 135790592 | bytes 4391936 | tf_op jit(solution)/shard_map/while/body/eval_jaxpr/hgrc,chd->rhgd/dot_general | solution.py:31
  58.0 2.6 %fusion.36 = (f32[4,8,8]{1,2,0:T(8,128)S(1)}, f32[4,8,8,2048]{3,1,2,0:T(8,128)S(1)}) fusion(bf16[2048,4,128,1]{2,1,0,3:T(4,128)(2,1)} %bitcast.53, pred[4,8,2048]{2,1,0:T(8,128)(4,1)S(1)} %compare_and_fusion.3, bf16[1,8,32,128]{3,1,2,0:T(8,128)(2,1)S(1)} %dynamic-slice_bitcast_fusion.3), kind=kOutput, calls=%fused_computation.31.clone.clone.1 | convolution fusion | flops 135790336 | bytes 4326400 | tf_op jit(solution)/shard_map/while/body/eval_jaxpr/rhgd,chd->hgrc/dot_general | solution.py:22
  61.3 2.4 %fusion.38 = f32[8,4,8,128]{3,2,0,1:T(8,128)S(1)} fusion(bf16[2048,4,128,1]{2,1,0,3:T(4,128)(2,1)} %bitcast.58, f32[4,8,8,2048]{3,1,2,0:T(8,128)S(1)} %get-tuple-element.231, f32[4,8,8]{1,2,0:T(8,128)S(1)} %get-tuple-element.232, pred[4,8,2048]{2,1,0:T(8,128)(4,1)S(1)} %compare_and_fusion.3), kind=kOutput, calls=%fused_computation.10.clone.clone.1 | convolution fusion | flops 135790592 | bytes 4391936 | tf_op jit(solution)/shard_map/while/body/eval_jaxpr/hgrc,chd->rhgd/dot_general | solution.py:31
  65.2 2.6 %fusion.36 = (f32[4,8,8]{1,2,0:T(8,128)S(1)}, f32[4,8,8,2048]{3,1,2,0:T(8,128)S(1)}) fusion(bf16[2048,4,128,1]{2,1,0,3:T(4,128)(2,1)} %bitcast.53, pred[4,8,2048]{2,1,0:T(8,128)(4,1)S(1)} %compare_and_fusion.3, bf16[1,8,32,128]{3,1,2,0:T(8,128)(2,1)S(1)} %dynamic-slice_bitcast_fusion.3), kind=kOutput, calls=%fused_computation.31.clone.clone.1 | convolution fusion | flops 135790336 | bytes 4326400 | tf_op jit(solution)/shard_map/while/body/eval_jaxpr/rhgd,chd->hgrc/dot_general | solution.py:22
  68.6 2.4 %fusion.38 = f32[8,4,8,128]{3,2,0,1:T(8,128)S(1)} fusion(bf16[2048,4,128,1]{2,1,0,3:T(4,128)(2,1)} %bitcast.58, f32[4,8,8,2048]{3,1,2,0:T(8,128)S(1)} %get-tuple-element.231, f32[4,8,8]{1,2,0:T(8,128)S(1)} %get-tuple-element.232, pred[4,8,2048]{2,1,0:T(8,128)(4,1)S(1)} %compare_and_fusion.3), kind=kOutput, calls=%fused_computation.10.clone.clone.1 | convolution fusion | flops 135790592 | bytes 4391936 | tf_op jit(solution)/shard_map/while/body/eval_jaxpr/hgrc,chd->rhgd/dot_general | solution.py:31
  72.5 2.6 %fusion.36 = (f32[4,8,8]{1,2,0:T(8,128)S(1)}, f32[4,8,8,2048]{3,1,2,0:T(8,128)S(1)}) fusion(bf16[2048,4,128,1]{2,1,0,3:T(4,128)(2,1)} %bitcast.53, pred[4,8,2048]{2,1,0:T(8,128)(4,1)S(1)} %compare_and_fusion.3, bf16[1,8,32,128]{3,1,2,0:T(8,128)(2,1)S(1)} %dynamic-slice_bitcast_fusion.3), kind=kOutput, calls=%fused_computation.31.clone.clone.1 | convolution fusion | flops 135790336 | bytes 4326400 | tf_op jit(solution)/shard_map/while/body/eval_jaxpr/rhgd,chd->hgrc/dot_general | solution.py:22
  75.9 2.4 %fusion.38 = f32[8,4,8,128]{3,2,0,1:T(8,128)S(1)} fusion(bf16[2048,4,128,1]{2,1,0,3:T(4,128)(2,1)} %bitcast.58, f32[4,8,8,2048]{3,1,2,0:T(8,128)S(1)} %get-tuple-element.231, f32[4,8,8]{1,2,0:T(8,128)S(1)} %get-tuple-element.232, pred[4,8,2048]{2,1,0:T(8,128)(4,1)S(1)} %compare_and_fusion.3), kind=kOutput, calls=%fused_computation.10.clone.clone.1 | convolution fusion | flops 135790592 | bytes 4391936 | tf_op jit(solution)/shard_map/while/body/eval_jaxpr/hgrc,chd->rhgd/dot_general | solution.py:31
  79.8 2.6 %fusion.36 = (f32[4,8,8]{1,2,0:T(8,128)S(1)}, f32[4,8,8,2048]{3,1,2,0:T(8,128)S(1)}) fusion(bf16[2048,4,128,1]{2,1,0,3:T(4,128)(2,1)} %bitcast.53, pred[4,8,2048]{2,1,0:T(8,128)(4,1)S(1)} %compare_and_fusion.3, bf16[1,8,32,128]{3,1,2,0:T(8,128)(2,1)S(1)} %dynamic-slice_bitcast_fusion.3), kind=kOutput, calls=%fused_computation.31.clone.clone.1 | convolution fusion | flops 135790336 | bytes 4326400 | tf_op jit(solution)/shard_map/while/body/eval_jaxpr/rhgd,chd->hgrc/dot_general | solution.py:22
  83.2 2.4 %fusion.38 = f32[8,4,8,128]{3,2,0,1:T(8,128)S(1)} fusion(bf16[2048,4,128,1]{2,1,0,3:T(4,128)(2,1)} %bitcast.58, f32[4,8,8,2048]{3,1,2,0:T(8,128)S(1)} %get-tuple-element.231, f32[4,8,8]{1,2,0:T(8,128)S(1)} %get-tuple-element.232, pred[4,8,2048]{2,1,0:T(8,128)(4,1)S(1)} %compare_and_fusion.3), kind=kOutput, calls=%fused_computation.10.clone.clone.1 | convolution fusion | flops 135790592 | bytes 4391936 | tf_op jit(solution)/shard_map/while/body/eval_jaxpr/hgrc,chd->rhgd/dot_general | solution.py:31
  87.1 2.6 %fusion.36 = (f32[4,8,8]{1,2,0:T(8,128)S(1)}, f32[4,8,8,2048]{3,1,2,0:T(8,128)S(1)}) fusion(bf16[2048,4,128,1]{2,1,0,3:T(4,128)(2,1)} %bitcast.53, pred[4,8,2048]{2,1,0:T(8,128)(4,1)S(1)} %compare_and_fusion.3, bf16[1,8,32,128]{3,1,2,0:T(8,128)(2,1)S(1)} %dynamic-slice_bitcast_fusion.3), kind=kOutput, calls=%fused_computation.31.clone.clone.1 | convolution fusion | flops 135790336 | bytes 4326400 | tf_op jit(solution)/shard_map/while/body/eval_jaxpr/rhgd,chd->hgrc/dot_general | solution.py:22
  90.5 2.4 %fusion.38 = f32[8,4,8,128]{3,2,0,1:T(8,128)S(1)} fusion(bf16[2048,4,128,1]{2,1,0,3:T(4,128)(2,1)} %bitcast.58, f32[4,8,8,2048]{3,1,2,0:T(8,128)S(1)} %get-tuple-element.231, f32[4,8,8]{1,2,0:T(8,128)S(1)} %get-tuple-element.232, pred[4,8,2048]{2,1,0:T(8,128)(4,1)S(1)} %compare_and_fusion.3), kind=kOutput, calls=%fused_computation.10.clone.clone.1 | convolution fusion | flops 135790592 | bytes 4391936 | tf_op jit(solution)/shard_map/while/body/eval_jaxpr/hgrc,chd->rhgd/dot_general | solution.py:31
  94.4 2.6 %fusion.36 = (f32[4,8,8]{1,2,0:T(8,128)S(1)}, f32[4,8,8,2048]{3,1,2,0:T(8,128)S(1)}) fusion(bf16[2048,4,128,1]{2,1,0,3:T(4,128)(2,1)} %bitcast.53, pred[4,8,2048]{2,1,0:T(8,128)(4,1)S(1)} %compare_and_fusion.3, bf16[1,8,32,128]{3,1,2,0:T(8,128)(2,1)S(1)} %dynamic-slice_bitcast_fusion.3), kind=kOutput, calls=%fused_computation.31.clone.clone.1 | convolution fusion | flops 135790336 | bytes 4326400 | tf_op jit(solution)/shard_map/while/body/eval_jaxpr/rhgd,chd->hgrc/dot_general | solution.py:22
  97.8 2.4 %fusion.38 = f32[8,4,8,128]{3,2,0,1:T(8,128)S(1)} fusion(bf16[2048,4,128,1]{2,1,0,3:T(4,128)(2,1)} %bitcast.58, f32[4,8,8,2048]{3,1,2,0:T(8,128)S(1)} %get-tuple-element.231, f32[4,8,8]{1,2,0:T(8,128)S(1)} %get-tuple-element.232, pred[4,8,2048]{2,1,0:T(8,128)(4,1)S(1)} %compare_and_fusion.3), kind=kOutput, calls=%fused_computation.10.clone.clone.1 | convolution fusion | flops 135790592 | bytes 4391936 | tf_op jit(solution)/shard_map/while/body/eval_jaxpr/hgrc,chd->rhgd/dot_general | solution.py:31
  100.9 0.7 reshape.67
  101.6 3.5 %all-to-all-start.2 = ((f32[16,1,128]{2,1,0:T(1,128)}), f32[16,1,128]{2,1,0:T(1,128)S(1)}, u32[]{:S(2)}, u32[]{:S(2)}) async-start(f32[16,1,128]{2,1,0:T(1,128)} %reshape.67), calls=%async_computation.2 | async-start | bytes 16384 | tf_op jit(solution)/shard_map/all_to_all | solution.py:69
  105.0 0.7 reshape.65
  105.7 5.6 %all-to-all-done.2 = f32[16,1,128]{2,1,0:T(1,128)S(1)} async-done(((f32[16,1,128]{2,1,0:T(1,128)}), f32[16,1,128]{2,1,0:T(1,128)S(1)}, u32[]{:S(2)}, u32[]{:S(2)}) %all-to-all-start.2) | async-done | bytes 8224 | tf_op jit(solution)/shard_map/all_to_all | solution.py:69
  111.4 3.5 %all-to-all-start.1 = ((f32[16,1,128]{2,1,0:T(1,128)}), f32[16,1,128]{2,1,0:T(1,128)S(1)}, u32[]{:S(2)}, u32[]{:S(2)}) async-start(f32[16,1,128]{2,1,0:T(1,128)} %reshape.65), calls=%async_computation.1 | async-start | bytes 16384 | tf_op jit(solution)/shard_map/all_to_all | solution.py:69
  114.9 2.5 %reshape.49 = f32[16,4,4096]{2,1,0:T(4,128)} reshape(f32[8,8,4096]{2,1,0:T(8,128)} %get-tuple-element.59) | data formatting | bytes 2097152 | tf_op jit(solution)/shard_map/reshape | solution.py:68
  117.4 3.9 %all-to-all-done.1 = f32[16,1,128]{2,1,0:T(1,128)S(1)} async-done(((f32[16,1,128]{2,1,0:T(1,128)}), f32[16,1,128]{2,1,0:T(1,128)S(1)}, u32[]{:S(2)}, u32[]{:S(2)}) %all-to-all-start.1) | async-done | bytes 8224 | tf_op jit(solution)/shard_map/all_to_all | solution.py:69
  121.3 3.7 %all-to-all-start = ((f32[16,4,4096]{2,1,0:T(4,128)}), f32[16,4,4096]{2,1,0:T(4,128)S(1)}, u32[]{:S(2)}, u32[]{:S(2)}) async-start(f32[16,4,4096]{2,1,0:T(4,128)} %reshape.49), calls=%async_computation | async-start | bytes 2097152 | tf_op jit(solution)/shard_map/all_to_all | solution.py:69
  127.8 20.0 %all-to-all-done = f32[16,4,4096]{2,1,0:T(4,128)S(1)} async-done(((f32[16,4,4096]{2,1,0:T(4,128)}), f32[16,4,4096]{2,1,0:T(4,128)S(1)}, u32[]{:S(2)}, u32[]{:S(2)}) %all-to-all-start) | async-done | bytes 1048608 | tf_op jit(solution)/shard_map/all_to_all | solution.py:69
  (126 shorter events, 22.3 us)
Async XLA Ops:
  36.4 4.1 %copy-start = (bf16[2048,512]{1,0:T(8,128)(2,1)S(1)}, bf16[2048,512]{1,0:T(8,128)(2,1)}, u32[]{:S(2)}) copy-start(bf16[2048,512]{1,0:T(8,128)(2,1)} %param.10) | copy-start | bytes 6291460
  40.6 2.0 %copy-start.1 = (s32[2048]{0:T(1024)S(1)}, s32[2048]{0:T(1024)}, u32[]{:S(2)}) copy-start(s32[2048]{0:T(1024)} %param.11) | copy-start | bytes 24580
  101.6 9.8 %all-to-all-start.2 = ((f32[16,1,128]{2,1,0:T(1,128)}), f32[16,1,128]{2,1,0:T(1,128)S(1)}, u32[]{:S(2)}, u32[]{:S(2)}) async-start(f32[16,1,128]{2,1,0:T(1,128)} %reshape.67), calls=%async_computation.2 | async-start | bytes 16384 | tf_op jit(solution)/shard_map/all_to_all | solution.py:69
  111.4 9.9 %all-to-all-start.1 = ((f32[16,1,128]{2,1,0:T(1,128)}), f32[16,1,128]{2,1,0:T(1,128)S(1)}, u32[]{:S(2)}, u32[]{:S(2)}) async-start(f32[16,1,128]{2,1,0:T(1,128)} %reshape.65), calls=%async_computation.1 | async-start | bytes 16384 | tf_op jit(solution)/shard_map/all_to_all | solution.py:69
  121.3 26.5 %all-to-all-start = ((f32[16,4,4096]{2,1,0:T(4,128)}), f32[16,4,4096]{2,1,0:T(4,128)S(1)}, u32[]{:S(2)}, u32[]{:S(2)}) async-start(f32[16,4,4096]{2,1,0:T(4,128)} %reshape.49), calls=%async_computation | async-start | bytes 2097152 | tf_op jit(solution)/shard_map/all_to_all | solution.py:69
where the time goes:
time: 151 us; the launch traced here: 149 us
  matrix products  39.6 us (26%)
  blocking collectives  33.3 us (22%)
  waiting for transfers between devices  29.5 us (20%)
  local copies, waits for them, and re-layouts  21.1 us (14%)
  other arithmetic  13.4 us (9%)
  starting transfers between devices  10.6 us (7%)
    all_to_all x3, waiting for transfers between devices, per_device(): home = lax.all_to_all(parts, 'ctx', split_axis=0, concat_axis=0, tiled=True)  29.5 us
    dot_general x8, matrix products, attend_block(): jnp.einsum('rhgd,chd->hgrc', q_split, k_split, preferred_element_type=jnp...  20.6 us
    all_gather x1, blocking collectives, per_device(): everyone = lax.all_gather(queries, 'ctx', axis=0, tiled=True)  19.6 us
    dot_general x8, matrix products, attend_block(): jnp.einsum('hgrc,chd->rhgd', weights.astype(jnp.bfloat16), v_split, prefe...  19 us
    unnamed x1, blocking collectives  13.7 us
    all_to_all x3, starting transfers between devices, per_device(): home = lax.all_to_all(parts, 'ctx', split_axis=0, concat_axis=0, tiled=True)  10.6 us
    dynamic_update_slice x16, local copies, waits for them, and re-layouts, per_device(): lax.map(one_block, (everyone.reshape(turns, span, everyone.shape[1]), eve...  5.35 us
    lt x8, other arithmetic, per_device(): live_slots = jnp.arange(keys.shape[0], dtype=jnp.int32) < lengths[0]  5.2 us
  transfers between devices with their start and end apart: 3, of which 3 were waited for; matrix products, arithmetic and copies ran while one was open for 4% of the time, Pallas kernels for 0%

commit v1 on v0

v1 whole, which is shorter than its diff:
```python
import functools
import math

import jax
import jax.numpy as jnp
from jax import lax
from jax.experimental import pallas as pl
from jax.experimental.pallas import tpu as pltpu
from jax.sharding import PartitionSpec as P

HD = 128
GROUP = 8
SUB = 8
NEG_FILL = -1e30
FAR = 2**30
EXP_SCALE = math.log2(math.e) * HD**-0.5


def kernel(
    n,
    lengths_ref, places_ref, queries_ref, slots_ref, keys_ref, values_ref, out_ref,
    heads_f32, q_mine, q_all, p_mine, p_all, k_buf, v_buf, s_buf, bias, o_mine, o_all,
    st_mine, st_all, w_rows, w_cols,
    k_sem, v_sem, pair_send, pair_recv,
    q_send, q_recv, p_send, p_recv, o_send, o_recv, st_send, st_recv,
):
    tok = queries_ref.shape[0]
    rows = tok * GROUP
    slots = keys_ref.shape[0]
    kv_local = keys_ref.shape[1] // HD
    half = kv_local // 2
    width = half * HD
    per = HD // rows
    batches = n // per

    me = lax.axis_index("ctx")
    core = lax.rem(me, 2)
    twin = me + 1 - 2 * core
    my_batch = lax.div(me, per)
    my_place = lax.rem(me, per)

    def to(device):
        return {"ctx": device}

    def remote(src, dst, send, recv, device):
        return pltpu.make_async_remote_copy(
            src_ref=src, dst_ref=dst, send_sem=send, recv_sem=recv,
            device_id=to(device), device_id_type=pl.DeviceIdType.MESH,
        )

    mine_cols = pl.ds(pl.multiple_of(core * width, HD), width)
    twin_cols = pl.ds(pl.multiple_of((1 - core) * width, HD), width)
    own_k = pltpu.make_async_copy(keys_ref.at[:, mine_cols], k_buf.at[0], k_sem)
    own_v = pltpu.make_async_copy(values_ref.at[:, mine_cols], v_buf.at[0], v_sem)

    barrier = pltpu.get_barrier_semaphore()
    for step in range(1, n):
        pl.semaphore_signal(
            barrier, inc=1, device_id=to(lax.rem(me + step, n)),
            device_id_type=pl.DeviceIdType.MESH,
        )
    own_k.start()
    own_v.start()

    wide = queries_ref[...].astype(jnp.float32)
    for kv in range(kv_local):
        for g in range(GROUP):
            col = (kv * GROUP + g) * HD
            heads_f32[kv, g * tok:(g + 1) * tok, :] = wide[:, col:col + HD]
    for c in range(2):
        for h in range(half):
            q_mine[c, h] = heads_f32[c * half + h].astype(jnp.bfloat16)
    sub = lax.rem(lax.broadcasted_iota(jnp.int32, (SUB, HD), 0), tok)
    place = jnp.full((SUB, HD), places_ref[0], jnp.int32)
    for t in range(1, tok):
        place = jnp.where(sub == t, places_ref[t], place)
    p_mine[...] = place
    p_all[me] = place
    q_all[me] = q_mine[core]
    live = lax.broadcasted_iota(jnp.int32, (1, slots), 1) < lengths_ref[0]
    s_buf[0] = jnp.where(live, slots_ref[...], FAR)

    pl.semaphore_wait(barrier, n - 1)

    pair = [
        remote(s_buf.at[0], s_buf.at[1], pair_send.at[0], pair_recv.at[0], twin),
        remote(keys_ref.at[:, twin_cols], k_buf.at[1], pair_send.at[1], pair_recv.at[1], twin),
        remote(values_ref.at[:, twin_cols], v_buf.at[1], pair_send.at[2], pair_recv.at[2], twin),
    ]

    def q_copy(peer, slot):
        return remote(q_mine.at[lax.rem(peer, 2)], q_all.at[slot], q_send.at[peer], q_recv.at[slot], peer)

    def p_copy(peer, slot):
        return remote(p_mine, p_all.at[slot], p_send.at[peer], p_recv.at[slot], peer)

    def peer_at(back, j):
        group = lax.rem(my_batch + batches - back, batches)
        return group * per + lax.rem(my_place + j, per)

    for back in range(batches):
        for j in range(per):
            if back == 0 and j == 0:
                continue
            peer = peer_at(back, j)
            p_copy(peer, me).start()
            q_copy(peer, me).start()
        if back == 0:
            for copy in pair:
                copy.start()

    own_k.wait()
    own_v.wait()
    for copy in pair:
        copy.wait()

    def o_copy(peer, slot):
        return remote(o_mine.at[peer], o_all.at[slot], o_send.at[peer], o_recv.at[slot], peer)

    def st_copy(peer, slot):
        return remote(
            st_mine.at[lax.div(peer, per)], st_all.at[slot], st_send.at[peer], st_recv.at[slot], peer
        )

    def one_batch(ahead, carry):
        group = lax.rem(my_batch + ahead, batches)
        first = group * per
        for j in range(per):
            src = first + j

            @pl.when(src != me)
            def _():
                p_copy(src, src).wait_recv()
                q_copy(src, src).wait_recv()

        for j in range(per):
            at = p_all[first + j]
            for side in range(2):
                far = jnp.concatenate([at] * (slots // HD), axis=1)
                seen = jnp.broadcast_to(s_buf[side], (SUB, slots)) <= far
                bias[j, :, side * slots:(side + 1) * slots] = jnp.where(seen, 0.0, NEG_FILL)

        lane = lax.broadcasted_iota(jnp.int32, (HD, HD), 1)
        stats = jnp.zeros((HD, HD), jnp.float32)
        for h in range(half):
            q = q_all[pl.ds(first, per), h].reshape(HD, HD)
            cols = slice(h * HD, (h + 1) * HD)
            keys = k_buf[:, :, cols].reshape(2 * slots, HD)
            vals = v_buf[:, :, cols].reshape(2 * slots, HD)
            s = lax.dot_general(
                q, keys, (((1,), (1,)), ((), ())), preferred_element_type=jnp.float32
            )
            s = s.reshape(per, rows // SUB, SUB, 2 * slots) + bias[...][:, None]
            s = s.reshape(HD, 2 * slots)
            top = jnp.max(s, axis=1, keepdims=True)
            w = jnp.exp2((s - top) * EXP_SCALE)
            total = jnp.sum(w, axis=1, keepdims=True)
            o = jnp.dot(w.astype(jnp.bfloat16), vals, preferred_element_type=jnp.float32)
            o_mine[pl.ds(first, per), h] = o.astype(jnp.bfloat16).reshape(per, rows, HD)
            stats = jnp.where(lane == h, top, stats)
            stats = jnp.where(lane == half + h, total, stats)
        st_mine[group] = stats.T[:SUB]

        for j in range(per):
            dst = first + lax.rem(my_place + j, per)

            @pl.when(dst != me)
            def _():
                st_copy(dst, me).start()
                o_copy(dst, me).start()

        return carry

    lax.fori_loop(0, batches, one_batch, 0)
    o_all[me] = o_mine[me]
    st_all[me] = st_mine[my_batch]

    for back in range(batches):
        for j in range(per):
            if back == 0 and j == 0:
                continue
            src = peer_at(back, j)
            st_copy(src, src).wait_recv()
            o_copy(src, src).wait_recv()

    for c in range(2):
        members = range(c, n, 2)
        top = functools.reduce(jnp.maximum, [st_all[s, :half] for s in members])
        factors = [jnp.exp2((st_all[s, :half] - top) * EXP_SCALE) for s in members]
        total = functools.reduce(
            jnp.add, [st_all[s, half:2 * half] * f for s, f in zip(members, factors)]
        )
        inverse = 1.0 / total
        for s, f in zip(members, factors):
            w_rows[s * SUB:s * SUB + half, :] = f * inverse
    for at in range(0, n * SUB, HD):
        w_cols[:, at:at + HD] = w_rows[at:at + HD, :].T
    weight = w_cols[pl.ds(pl.multiple_of(my_place * rows, rows), rows), :]
    for c in range(2):
        for h in range(half):
            result = jnp.zeros((rows, HD), jnp.float32)
            for s in range(c, n, 2):
                col = s * SUB + h
                result = result + weight[:, col:col + 1] * o_all[s, h].astype(jnp.float32)
            heads_f32[c * half + h] = result
    for kv in range(kv_local):
        for g in range(GROUP):
            col = (kv * GROUP + g) * HD
            out_ref[:, col:col + HD] = heads_f32[kv, g * tok:(g + 1) * tok, :].astype(jnp.bfloat16)

    for back in range(batches):
        for j in range(per):
            if back == 0 and j == 0:
                continue
            peer = peer_at(back, j)
            p_copy(peer, me).wait_send()
            q_copy(peer, me).wait_send()
            st_copy(peer, me).wait_send()
            o_copy(peer, me).wait_send()


def per_device(n, queries, keys, values, cache_positions, query_positions, lengths):
    tok, wide = queries.shape
    slots = keys.shape[0]
    kv_local = keys.shape[1] // HD
    half = kv_local // 2
    rows = tok * GROUP
    per = HD // rows
    vmem = pl.BlockSpec(memory_space=pltpu.VMEM)
    smem = pl.BlockSpec(memory_space=pltpu.SMEM)
    hbm = pl.BlockSpec(memory_space=pltpu.HBM)
    dma = pltpu.SemaphoreType.DMA
    return pl.pallas_call(
        functools.partial(kernel, n),
        out_shape=jax.ShapeDtypeStruct((tok, wide), jnp.bfloat16),
        in_specs=[smem, smem, vmem, vmem, hbm, hbm],
        out_specs=vmem,
        scratch_shapes=[
            pltpu.VMEM((kv_local, rows, HD), jnp.float32),
            pltpu.VMEM((2, half, rows, HD), jnp.bfloat16),
            pltpu.VMEM((n, half, rows, HD), jnp.bfloat16),
            pltpu.VMEM((SUB, HD), jnp.int32),
            pltpu.VMEM((n, SUB, HD), jnp.int32),
            pltpu.VMEM((2, slots, half * HD), jnp.bfloat16),
            pltpu.VMEM((2, slots, half * HD), jnp.bfloat16),
            pltpu.VMEM((2, 1, slots), jnp.int32),
            pltpu.VMEM((per, SUB, 2 * slots), jnp.float32),
            pltpu.VMEM((n, half, rows, HD), jnp.bfloat16),
            pltpu.VMEM((n, half, rows, HD), jnp.bfloat16),
            pltpu.VMEM((n // per, SUB, HD), jnp.float32),
            pltpu.VMEM((n, SUB, HD), jnp.float32),
            pltpu.VMEM((n * SUB, HD), jnp.float32),
            pltpu.VMEM((HD, n * SUB), jnp.float32),
            dma, dma, dma((3,)), dma((3,)),
            dma((n,)), dma((n,)), dma((n,)), dma((n,)),
            dma((n,)), dma((n,)), dma((n,)), dma((n,)),
        ],
        compiler_params=pltpu.CompilerParams(
            collective_id=0, has_side_effects=True, vmem_limit_bytes=60 * 2**20
        ),
    )(lengths, query_positions, queries, cache_positions.reshape(1, slots), keys, values)


def solution(mesh):
    in_specs = (
        P("ctx", "heads"),
        P("ctx", "heads"),
        P("ctx", "heads"),
        P("ctx"),
        P("ctx"),
        P("ctx"),
    )
    return jax.shard_map(
        functools.partial(per_device, mesh.shape["ctx"]),
        mesh=mesh, in_specs=in_specs, out_specs=P("ctx", "heads"), check_vma=False,
    )
```

time: 151 us -> 28.8 us (0.19); the launches traced: 149 us -> 28.5 us
  matrix products: 39.6 us -> 0 us
  blocking collectives: 33.3 us -> 0 us
  waiting for transfers between devices: 29.5 us -> 0 us
  Pallas kernels: 0 us -> 26.5 us
  local copies, waits for them, and re-layouts: 21.1 us -> 1.39 us
  other arithmetic: 13.4 us -> 0 us
  starting transfers between devices: 10.6 us -> 0 us
    dot_general x16 -> x0, matrix products: 39.6 us -> none  [the longest x8 20.6 us: attend_block(): jnp.einsum('rhgd,chd->hgrc', q_split, k_split, preferred_element_type=jnp...]
    all_to_all x3 -> x0, waiting for transfers between devices: 29.5 us -> none  [per_device(): home = lax.all_to_all(parts, 'ctx', split_axis=0, concat_axis=0, tiled=True)]
    pallas_call x0 -> x1, Pallas kernels: none -> 26.5 us  [per_device(): pl.pallas_call(functools.partial(kernel, n), out_shape=jax.ShapeDtypeStru...]
    all_gather x1 -> x0, blocking collectives: 19.6 us -> none  [per_device(): everyone = lax.all_gather(queries, 'ctx', axis=0, tiled=True)]
    unnamed x1 -> x0, blocking collectives: 13.7 us -> none
    all_to_all x3 -> x0, starting transfers between devices: 10.6 us -> none  [per_device(): home = lax.all_to_all(parts, 'ctx', split_axis=0, concat_axis=0, tiled=True)]
    reshape x5 -> x0, local copies, waits for them, and re-layouts: 8.88 us -> none  [the longest x1 4.12 us: attend_block(): k_split = keys.reshape(cache_rows, kv_local, HD)]
    reduce_sum x10 -> x0, other arithmetic: 5.45 us -> none  [the longest x8 5.13 us: attend_block(): row_sum = jnp.sum(weights, axis=3)]
  transfers between devices with their start and end apart: 3 -> 0, of which waited for: 3 -> 0; matrix products, arithmetic and copies ran while one was open for 4% -> 0% of each run, Pallas kernels for 0% -> 0%
where the time goes in v1:
time: 28.8 us; the launch traced here: 28.5 us
  Pallas kernels  26.5 us (92%)
  local copies, waits for them, and re-layouts  1.39 us (5%)
  between operations  0.66 us (2%)
    pallas_call x1, Pallas kernels, per_device(): pl.pallas_call(functools.partial(kernel, n), out_shape=jax.ShapeDtypeStru...  26.5 us
    unnamed x1, local copies, waits for them, and re-layouts  1.39 us

profile of v1, /device:TPU:0, one launch (start us, length us, event | category | flops | bytes accessed | tf_op | source)
XLA Modules:
  0.0 28.5 jit_solution(6854769151236562798)
XLA Ops:
  0.7 26.5 %shard_map.64 = bf16[4,4096]{1,0:T(4,128)(2,1)} custom-call(s32[1]{0:T(128)S(6)} %copy.8.lengths_ref, s32[4]{0:T(128)} %places_ref.1, bf16[4,4096]{1,0:T(4,128)(2,1)} %queries_ref.1, s32[1,2048]{1,0:T(1,128)} %bitcast.1, bf16[2048,512]{1,0:T(8,128)(2,1)} %keys_ref.1, bf16[2048,512]{1,0:T(8,128)(2,1)} %values_ref.1), custom_call_target="tpu_custom_call" | custom-call | tf_op jit(solution)/shard_map/pallas_call | solution.py:233
  27.1 1.4 %copy.9 = bf16[4,4096]{1,0:T(4,128)(2,1)} copy(bf16[4,4096]{1,0:T(4,128)(2,1)} %shard_map.64) | data formatting | bytes 65536

commit v2 on v1

--- a/solution.py
+++ b/solution.py
@@ -12,16 +12,16 @@
 GROUP = 8
 SUB = 8
 NEG_FILL = -1e30
-FAR = 2**30
+FAR = 2.0**30
 EXP_SCALE = math.log2(math.e) * HD**-0.5
 
 
 def kernel(
     n,
     lengths_ref, places_ref, queries_ref, slots_ref, keys_ref, values_ref, out_ref,
-    heads_f32, q_mine, q_all, p_mine, p_all, k_buf, v_buf, s_buf, bias, o_mine, o_all,
-    st_mine, st_all, w_rows, w_cols,
-    k_sem, v_sem, pair_send, pair_recv,
+    q_in, heads_f32, q_mine, q_all, p_mine, p_all, k_buf, v_buf, s_buf, bias, o_mine, o_all,
+    st_mine, st_all, w_rows,
+    q_sem, k_sem, v_sem, pair_send, pair_recv,
     q_send, q_recv, p_send, p_recv, o_send, o_recv, st_send, st_recv,
 ):
     tok = queries_ref.shape[0]
@@ -53,16 +53,29 @@
     own_k = pltpu.make_async_copy(keys_ref.at[:, mine_cols], k_buf.at[0], k_sem)
     own_v = pltpu.make_async_copy(values_ref.at[:, mine_cols], v_buf.at[0], v_sem)
 
+    own_step = batches - 1
     barrier = pltpu.get_barrier_semaphore()
     for step in range(1, n):
         pl.semaphore_signal(
             barrier, inc=1, device_id=to(lax.rem(me + step, n)),
             device_id_type=pl.DeviceIdType.MESH,
         )
+    own_q = pltpu.make_async_copy(queries_ref, q_in, q_sem)
+    own_q.start()
     own_k.start()
     own_v.start()
 
-    wide = queries_ref[...].astype(jnp.float32)
+    lane_row = lax.broadcasted_iota(jnp.int32, (1, HD), 1)
+    place = jnp.zeros((1, HD), jnp.float32)
+    for t in range(tok):
+        place = jnp.where(lane_row == t, places_ref[t].astype(jnp.float32), place)
+    p_mine[...] = place
+    p_all[me] = place
+    live = lax.broadcasted_iota(jnp.int32, (1, slots), 1) < lengths_ref[0]
+    s_buf[0] = jnp.where(live, slots_ref[...].astype(jnp.float32), FAR)
+
+    own_q.wait()
+    wide = q_in[...].astype(jnp.float32)
     for kv in range(kv_local):
         for g in range(GROUP):
             col = (kv * GROUP + g) * HD
@@ -70,16 +83,7 @@
     for c in range(2):
         for h in range(half):
             q_mine[c, h] = heads_f32[c * half + h].astype(jnp.bfloat16)
-    sub = lax.rem(lax.broadcasted_iota(jnp.int32, (SUB, HD), 0), tok)
-    place = jnp.full((SUB, HD), places_ref[0], jnp.int32)
-    for t in range(1, tok):
-        place = jnp.where(sub == t, places_ref[t], place)
-    p_mine[...] = place
-    p_all[me] = place
     q_all[me] = q_mine[core]
-    live = lax.broadcasted_iota(jnp.int32, (1, slots), 1) < lengths_ref[0]
-    s_buf[0] = jnp.where(live, slots_ref[...], FAR)
-
     pl.semaphore_wait(barrier, n - 1)
 
     pair = [
@@ -94,13 +98,22 @@
     def p_copy(peer, slot):
         return remote(p_mine, p_all.at[slot], p_send.at[peer], p_recv.at[slot], peer)
 
-    def peer_at(back, j):
-        group = lax.rem(my_batch + batches - back, batches)
+    def group_of(step):
+        group, bit = my_batch, 1
+        while bit < batches:
+            mine = lax.rem(lax.div(my_batch, bit), 2)
+            other = lax.rem(lax.div(step + 1, bit), 2)
+            group = group + bit * other * (1 - 2 * mine)
+            bit *= 2
+        return group
+
+    def peer_at(step, j):
+        group = group_of(step)
         return group * per + lax.rem(my_place + j, per)
 
     for back in range(batches):
         for j in range(per):
-            if back == 0 and j == 0:
+            if back == own_step and j == 0:
                 continue
             peer = peer_at(back, j)
             p_copy(peer, me).start()
@@ -119,11 +132,16 @@
 
     def st_copy(peer, slot):
         return remote(
-            st_mine.at[lax.div(peer, per)], st_all.at[slot], st_send.at[peer], st_recv.at[slot], peer
+            st_mine.at[peer], st_all.at[slot], st_send.at[peer], st_recv.at[slot], peer
         )
 
+    lane = lax.broadcasted_iota(jnp.int32, (HD, HD), 1)
+    token_lane = lax.broadcasted_iota(jnp.int32, (SUB, HD), 1) == lax.rem(
+        lax.broadcasted_iota(jnp.int32, (SUB, HD), 0), tok
+    )
+
     def one_batch(ahead, carry):
-        group = lax.rem(my_batch + ahead, batches)
+        group = group_of(ahead)
         first = group * per
         for j in range(per):
             src = first + j
@@ -134,14 +152,13 @@
                 q_copy(src, src).wait_recv()
 
         for j in range(per):
-            at = p_all[first + j]
+            row = jnp.broadcast_to(p_all[first + j], (SUB, HD))
+            at = jnp.max(jnp.where(token_lane, row, -1.0), axis=1, keepdims=True)
             for side in range(2):
-                far = jnp.concatenate([at] * (slots // HD), axis=1)
-                seen = jnp.broadcast_to(s_buf[side], (SUB, slots)) <= far
+                seen = jnp.broadcast_to(s_buf[side], (SUB, slots)) <= at
                 bias[j, :, side * slots:(side + 1) * slots] = jnp.where(seen, 0.0, NEG_FILL)
 
-        lane = lax.broadcasted_iota(jnp.int32, (HD, HD), 1)
-        stats = jnp.zeros((HD, HD), jnp.float32)
+        tops, sums = [], []
         for h in range(half):
             q = q_all[pl.ds(first, per), h].reshape(HD, HD)
             cols = slice(h * HD, (h + 1) * HD)
@@ -157,9 +174,15 @@
             total = jnp.sum(w, axis=1, keepdims=True)
             o = jnp.dot(w.astype(jnp.bfloat16), vals, preferred_element_type=jnp.float32)
             o_mine[pl.ds(first, per), h] = o.astype(jnp.bfloat16).reshape(per, rows, HD)
-            stats = jnp.where(lane == h, top, stats)
-            stats = jnp.where(lane == half + h, total, stats)
-        st_mine[group] = stats.T[:SUB]
+            tops.append(top)
+            sums.append(total)
+        stats = jnp.zeros((HD, HD), jnp.float32)
+        for j in range(per):
+            column = jnp.concatenate([v[j * rows:(j + 1) * rows] for v in tops + sums], axis=0)
+            stats = jnp.where(lane == j, column, stats)
+        stats = stats.T
+        for j in range(per):
+            st_mine[first + j] = stats[j:j + 1]
 
         for j in range(per):
             dst = first + lax.rem(my_place + j, per)
@@ -171,37 +194,36 @@
 
         return carry
 
-    lax.fori_loop(0, batches, one_batch, 0)
+    lax.fori_loop(0, batches, one_batch, 0, unroll=min(batches, 4))
     o_all[me] = o_mine[me]
-    st_all[me] = st_mine[my_batch]
+    st_all[me] = st_mine[me]
 
     for back in range(batches):
         for j in range(per):
-            if back == 0 and j == 0:
+            if back == own_step and j == 0:
                 continue
             src = peer_at(back, j)
             st_copy(src, src).wait_recv()
             o_copy(src, src).wait_recv()
 
+    sources = n // 2
+    w_rows[...] = jnp.zeros_like(w_rows)
     for c in range(2):
-        members = range(c, n, 2)
-        top = functools.reduce(jnp.maximum, [st_all[s, :half] for s in members])
-        factors = [jnp.exp2((st_all[s, :half] - top) * EXP_SCALE) for s in members]
-        total = functools.reduce(
-            jnp.add, [st_all[s, half:2 * half] * f for s, f in zip(members, factors)]
-        )
-        inverse = 1.0 / total
-        for s, f in zip(members, factors):
-            w_rows[s * SUB:s * SUB + half, :] = f * inverse
-    for at in range(0, n * SUB, HD):
-        w_cols[:, at:at + HD] = w_rows[at:at + HD, :].T
-    weight = w_cols[pl.ds(pl.multiple_of(my_place * rows, rows), rows), :]
+        for b in range(sources):
+            w_rows[c * sources + b:c * sources + b + 1, :] = st_all[2 * b + c]
+    count = half * rows
+    spread = w_rows[...].T
     for c in range(2):
+        mine = spread[:, c * sources:(c + 1) * sources]
+        top = jnp.max(mine[:count], axis=1, keepdims=True)
+        factor = jnp.exp2((mine[:count] - top) * EXP_SCALE)
+        total = jnp.sum(mine[count:2 * count] * factor, axis=1, keepdims=True)
+        factor = factor / total
         for h in range(half):
+            span = slice(h * rows, (h + 1) * rows)
             result = jnp.zeros((rows, HD), jnp.float32)
-            for s in range(c, n, 2):
-                col = s * SUB + h
-                result = result + weight[:, col:col + 1] * o_all[s, h].astype(jnp.float32)
+            for b in range(sources):
+                result = result + factor[span, b:b + 1] * o_all[2 * b + c, h].astype(jnp.float32)
             heads_f32[c * half + h] = result
     for kv in range(kv_local):
         for g in range(GROUP):
@@ -210,7 +232,7 @@
 
     for back in range(batches):
         for j in range(per):
-            if back == 0 and j == 0:
+            if back == own_step and j == 0:
                 continue
             peer = peer_at(back, j)
             p_copy(peer, me).wait_send()
@@ -233,25 +255,25 @@
     return pl.pallas_call(
         functools.partial(kernel, n),
         out_shape=jax.ShapeDtypeStruct((tok, wide), jnp.bfloat16),
-        in_specs=[smem, smem, vmem, vmem, hbm, hbm],
+        in_specs=[smem, smem, hbm, vmem, hbm, hbm],
         out_specs=vmem,
         scratch_shapes=[
+            pltpu.VMEM((tok, wide), jnp.bfloat16),
             pltpu.VMEM((kv_local, rows, HD), jnp.float32),
             pltpu.VMEM((2, half, rows, HD), jnp.bfloat16),
             pltpu.VMEM((n, half, rows, HD), jnp.bfloat16),
-            pltpu.VMEM((SUB, HD), jnp.int32),
-            pltpu.VMEM((n, SUB, HD), jnp.int32),
+            pltpu.VMEM((1, HD), jnp.float32),
+            pltpu.VMEM((n, 1, HD), jnp.float32),
             pltpu.VMEM((2, slots, half * HD), jnp.bfloat16),
             pltpu.VMEM((2, slots, half * HD), jnp.bfloat16),
-            pltpu.VMEM((2, 1, slots), jnp.int32),
+            pltpu.VMEM((2, 1, slots), jnp.float32),
             pltpu.VMEM((per, SUB, 2 * slots), jnp.float32),
             pltpu.VMEM((n, half, rows, HD), jnp.bfloat16),
             pltpu.VMEM((n, half, rows, HD), jnp.bfloat16),
-            pltpu.VMEM((n // per, SUB, HD), jnp.float32),
-            pltpu.VMEM((n, SUB, HD), jnp.float32),
-            pltpu.VMEM((n * SUB, HD), jnp.float32),
-            pltpu.VMEM((HD, n * SUB), jnp.float32),
-            dma, dma, dma((3,)), dma((3,)),
+            pltpu.VMEM((n, 1, HD), jnp.float32),
+            pltpu.VMEM((n, 1, HD), jnp.float32),
+            pltpu.VMEM((pl.cdiv(n, HD) * HD, HD), jnp.float32),
+            dma, dma, dma, dma((3,)), dma((3,)),
             dma((n,)), dma((n,)), dma((n,)), dma((n,)),
             dma((n,)), dma((n,)), dma((n,)), dma((n,)),
         ],

time: 28.8 us -> 27.6 us (0.958)
  Pallas kernels: 26.5 us -> 25.3 us
    pallas_call x1, Pallas kernels: 26.5 us -> 25.3 us  [per_device(): pl.pallas_call(functools.partial(kernel, n), out_shape=jax.ShapeDtypeStru...]
where the time goes in v2:
time: 27.6 us; the launch traced here: 27.4 us
  Pallas kernels  25.3 us (92%)
  local copies, waits for them, and re-layouts  1.39 us (5%)
  between operations  0.66 us (2%)
    pallas_call x1, Pallas kernels, per_device(): pl.pallas_call(functools.partial(kernel, n), out_shape=jax.ShapeDtypeStru...  25.3 us
    unnamed x1, local copies, waits for them, and re-layouts  1.39 us

profile of v2, /device:TPU:0, one launch (start us, length us, event | category | flops | bytes accessed | tf_op | source)
XLA Modules:
  0.0 27.4 jit_solution(12189583715244780456)
XLA Ops:
  0.7 25.3 %shard_map.64 = bf16[4,4096]{1,0:T(4,128)(2,1)} custom-call(s32[1]{0:T(128)S(6)} %copy.8.lengths_ref, s32[4]{0:T(128)} %places_ref.1, bf16[4,4096]{1,0:T(4,128)(2,1)} %queries_ref.1, s32[1,2048]{1,0:T(1,128)} %bitcast.1, bf16[2048,512]{1,0:T(8,128)(2,1)} %keys_ref.1, bf16[2048,512]{1,0:T(8,128)(2,1)} %values_ref.1), custom_call_target="tpu_custom_call" | custom-call | tf_op jit(solution)/shard_map/pallas_call | solution.py:255
  26.0 1.4 %copy.9 = bf16[4,4096]{1,0:T(4,128)(2,1)} copy(bf16[4,4096]{1,0:T(4,128)(2,1)} %shard_map.64) | data formatting | bytes 65536
